TPU v7x, 32 devices: a whole 2x2x4 slice. The times are simulated.
32 devices in a mesh: img: 2 (over x), ga: 4 (over y, core), band: 4 (over z).
Axes of the slice: x: 2, y: 2, z: 4, core: 2. Of those that a mesh axis runs over, the one named last changes fastest.
Arguments:
- orbitals: bfloat16 [1536, 12288], P(('img', 'band'), 'ga'), parts along dimension 0, as said below
- kernel: float32 [12288], P('ga'), may hold values from 0.3 to 3
- block_vectors: bfloat16 [512, 12288], P(('img', 'band'), 'ga'), parts along dimension 0
Outputs:
- ace_vectors: bfloat16 [1536, 12288], P(('img', 'band'), 'ga'), parts along dimension 0
- exchange_block: bfloat16 [512, 12288], P(('img', 'band'), 'ga'), parts along dimension 0
There are 2 independent parts, one for each index of `img`. A program takes and returns all parts, laid end to end along the dimension named above; an argument that names none is the same for every part. Nothing has to cross between parts.
Inputs may be any that keep to these rules, and one draw needn't show every extreme that they name: `orbitals`: the bands of one image are linearly independent, and the block lies largely in their span.
All inputs are finite; a program needn't handle non-finite values.
Results may differ from a plain program's by a relative error of at most 0.02.
Values may be sent and summed in bfloat16 or wider, within the bound.
A program may use at most 64 MiB of HBM per device.

v0:
```python
import jax
import jax.numpy as jnp
from jax import lax
from jax.sharding import PartitionSpec as P


def contract_first(left, right):
    return lax.dot_general(left, right, (((0,), (0,)), ((), ())), precision=lax.Precision.HIGHEST)


def shards(orbitals, kernel, block_vectors):
    groups = lax.axis_size("ga")
    own_band = lax.axis_index("band")
    total_coeffs = orbitals.shape[1] * groups
    full_orbitals, full_block = (
        lax.all_gather(orbitals, "band", axis=0, tiled=True),
        lax.all_gather(block_vectors, "band", axis=0, tiled=True),
    )
    weighted = (-(full_orbitals.astype(jnp.float32) * kernel[None, :])).astype(jnp.bfloat16)
    own_rows = orbitals.shape[0]
    partial_rows = lax.dot_general(
        orbitals, weighted, (((1,), (1,)), ((), ())), preferred_element_type=jnp.float32
    )
    summed_rows = lax.psum(partial_rows.astype(jnp.bfloat16), "ga").astype(jnp.float32)
    margin = -lax.all_gather(summed_rows, "band", axis=0, tiled=True) / total_coeffs
    factor = jnp.linalg.cholesky(margin)
    identity = jnp.eye(factor.shape[0], dtype=jnp.float32)
    inverse = lax.linalg.triangular_solve(factor, identity, left_side=True, lower=True)
    inverse_rows = lax.dynamic_slice_in_dim(inverse, own_band * own_rows, own_rows, 0)
    projector = jnp.dot(inverse_rows, weighted.astype(jnp.float32), precision=lax.Precision.HIGHEST)
    local_coupling = jnp.dot(
        projector, full_block.astype(jnp.float32).T, precision=lax.Precision.HIGHEST
    )
    coupling = (
        lax.psum(local_coupling.astype(jnp.bfloat16), "ga").astype(jnp.float32) / total_coeffs
    )
    applied = lax.psum_scatter(
        -contract_first(coupling, projector), "band", scatter_dimension=0, tiled=True
    )
    return (projector.astype(jnp.bfloat16), applied.astype(jnp.bfloat16))


def solution(mesh):
    placed = (P(("img", "band"), "ga"), P("ga"), P(("img", "band"), "ga"))
    return jax.shard_map(
        shards,
        mesh=mesh,
        in_specs=placed,
        out_specs=(P(("img", "band"), "ga"), P(("img", "band"), "ga")),
        check_vma=False,
    )
```

profile of v0, /device:TPU:0, one launch (start us, length us, event | category | flops | bytes accessed | tf_op | source)
XLA Modules:
  0.0 548.5 jit_solution(6717364289099904385)
XLA Ops:
  7.2 0.7 all-gather.4.cloned.1.call-update
  7.9 93.7 %all-gather.4.cloned.1.call-done = bf16[768,3072]{1,0:T(8,128)(2,1)} async-done(((bf16[192,3072]{1,0:T(8,128)(2,1)}), bf16[768,3072]{1,0:T(8,128)(2,1)}) %all-gather.4.cloned.1.call-update) | async-done | bytes 4718608 | tf_op jit(solution)/shard_map/all_gather | solution.py:16
  101.7 5.1 fusion.20
  106.9 30.9 %all-reduce.4.cloned.1.call-done = bf16[192,768]{1,0:T(8,128)(2,1)} async-done(((bf16[192,768]{1,0:T(8,128)(2,1)}), bf16[192,768]{1,0:T(8,128)(2,1)}) %all-reduce.4.cloned.1.call-update) | async-done | bytes 294928 | tf_op jit(solution)/shard_map/psum | solution.py:24
  137.8 1.8 convert_element_type.44
  140.5 1.6 fusion.24
  142.1 47.9 %all-gather.6.cloned.1.call-done = f32[768,768]{1,0:T(8,128)} async-done(((f32[192,768]{1,0:T(8,128)}), f32[768,768]{1,0:T(8,128)}) %all-gather.6.cloned.1.call-update) | async-done | bytes 2359312 | tf_op jit(solution)/shard_map/all_gather | solution.py:25
  190.0 2.0 copy.7
  192.1 1.7 negate_multiply_fusion
  193.7 3.2 copy.8
  197.0 2.1 fusion.2
  199.0 1.5 copy-done.1
  200.5 11.7 %cholesky.165 = f32[128,128]{1,0:T(8,128)S(1)} custom-call(f32[128,128]{1,0:T(8,128)S(1)} %cholesky.424), custom_call_target="Cholesky" | custom-call | tf_op jit(solution)/shard_map/jit(cholesky)/cholesky | solution.py:26
  212.3 9.8 %custom-call.46 = f32[1,128,128]{1,2,0:T(8,128)S(1)} custom-call(f32[1,128,128]{2,1,0:T(8,128)S(1)} %get-tuple-element.45), custom_call_target="InvertDiagBlocksLowerTriangular" | custom-call | tf_op jit(solution)/shard_map/jit(cholesky)/cholesky | solution.py:26
  222.2 1.4 constant_dynamic-update-slice_fusion.15
  223.6 1.4 convolution_subtract_fusion.4
  225.0 11.7 %cholesky.188 = f32[128,128]{1,0:T(8,128)S(1)} custom-call(f32[128,128]{1,0:T(8,128)S(1)} %cholesky.428), custom_call_target="Cholesky" | custom-call | tf_op jit(solution)/shard_map/jit(cholesky)/cholesky | solution.py:26
  236.8 10.0 %custom-call.47 = f32[1,128,128]{1,2,0:T(8,128)S(1)} custom-call(f32[1,128,128]{2,1,0:T(8,128)S(1)} %get-tuple-element.42), custom_call_target="InvertDiagBlocksLowerTriangular" | custom-call | tf_op jit(solution)/shard_map/jit(cholesky)/cholesky | solution.py:26
  247.2 1.5 convolution_subtract_fusion.5
  248.7 11.7 %cholesky.354 = f32[128,128]{1,0:T(8,128)S(1)} custom-call(f32[128,128]{1,0:T(8,128)S(1)} %cholesky.433), custom_call_target="Cholesky" | custom-call | tf_op jit(solution)/shard_map/jit(cholesky)/cholesky | solution.py:26
  260.5 0.7 compare_reduce_fusion.3
  261.2 9.8 %custom-call.48 = f32[1,128,128]{1,2,0:T(8,128)S(1)} custom-call(f32[1,128,128]{2,1,0:T(8,128)S(1)} %get-tuple-element.39), custom_call_target="InvertDiagBlocksLowerTriangular" | custom-call | tf_op jit(solution)/shard_map/jit(cholesky)/cholesky | solution.py:26
  271.3 1.6 convolution_subtract_fusion.6
  272.9 12.2 %cholesky.373 = f32[128,128]{1,0:T(8,128)S(1)} custom-call(f32[128,128]{1,0:T(8,128)S(1)} %cholesky.438), custom_call_target="Cholesky" | custom-call | tf_op jit(solution)/shard_map/jit(cholesky)/cholesky | solution.py:26
  285.1 0.7 compare_reduce_fusion.2
  285.8 9.8 %custom-call.49 = f32[1,128,128]{1,2,0:T(8,128)S(1)} custom-call(f32[1,128,128]{2,1,0:T(8,128)S(1)} %get-tuple-element.36), custom_call_target="InvertDiagBlocksLowerTriangular" | custom-call | tf_op jit(solution)/shard_map/jit(cholesky)/cholesky | solution.py:26
  295.9 1.5 convolution_subtract_fusion.7
  297.4 11.7 %cholesky.392 = f32[128,128]{1,0:T(8,128)S(1)} custom-call(f32[128,128]{1,0:T(8,128)S(1)} %cholesky.443), custom_call_target="Cholesky" | custom-call | tf_op jit(solution)/shard_map/jit(cholesky)/cholesky | solution.py:26
  309.1 0.7 compare_reduce_fusion.1
  309.8 9.8 %custom-call.50 = f32[1,128,128]{1,2,0:T(8,128)S(1)} custom-call(f32[1,128,128]{2,1,0:T(8,128)S(1)} %get-tuple-element.33), custom_call_target="InvertDiagBlocksLowerTriangular" | custom-call | tf_op jit(solution)/shard_map/jit(cholesky)/cholesky | solution.py:26
  319.9 1.3 convolution_subtract_fusion.8
  321.2 11.9 %cholesky.410 = f32[128,128]{1,0:T(8,128)S(1)} custom-call(f32[128,128]{1,0:T(8,128)S(1)} %convolution_subtract_fusion.8), custom_call_target="Cholesky" | custom-call | tf_op jit(solution)/shard_map/jit(cholesky)/cholesky | solution.py:26
  333.1 0.7 compare_reduce_fusion
  333.8 0.7 compare_reduce_fusion.4
  338.4 1.6 select_select_fusion
  340.0 21.3 %while.1 = (s32[]{:T(128)}, f32[768,768]{1,0:T(8,128)}, s32[6,2]{0,1:T(2,128)S(1)}, f32[6,128,128]{2,1,0:T(8,128)}, s32[]{:T(128)}) while((s32[]{:T(128)}, f32[768,768]{1,0:T(8,128)}, s32[6,2]{0,1:T(2,128)S(1)}, f32[6,128,128]{2,1,0:T(8,128)}, s32[]{:T(128)}) %tuple.45), condition=%wide.while_cond, body=%wide.while_body.sunk | while | flops 2 | bytes 132705 | solution.py:28
  340.1 0.6 fusion.79
  340.6 3.0 bitcast_dynamic-update-slice_fusion.2
  343.7 0.6 fusion.79
  344.3 2.9 bitcast_dynamic-update-slice_fusion.2
  347.2 0.6 fusion.79
  347.8 2.9 bitcast_dynamic-update-slice_fusion.2
  350.8 0.6 fusion.79
  351.4 2.9 bitcast_dynamic-update-slice_fusion.2
  354.3 0.6 fusion.79
  354.9 2.9 bitcast_dynamic-update-slice_fusion.2
  357.9 0.6 fusion.79
  358.4 2.8 bitcast_dynamic-update-slice_fusion.2
  361.3 60.4 %custom-call.51 = f32[6,128,128]{1,2,0:T(8,128)} custom-call(f32[6,128,128]{2,1,0:T(8,128)} %get-tuple-element.9), custom_call_target="InvertDiagBlocksLowerTriangular" | custom-call | tf_op jit(solution)/shard_map/triangular_solve | solution.py:28
  421.7 1.3 constant_dynamic-update-slice_fusion.4
  423.0 1.5 convolution_subtract_fusion.2
  424.5 0.5 constant_dynamic-update-slice_fusion.3
  425.1 1.5 convolution_subtract_fusion.3
  426.5 0.5 constant_dynamic-update-slice_fusion.2
  427.1 2.0 convolution_subtract_fusion.1
  429.1 0.5 constant_dynamic-update-slice_fusion.1
  429.6 2.0 fusion.12
  432.2 2.3 convolution_subtract_fusion
  435.0 4.2 fusion.65
  439.3 3.8 convolution_convert_fusion
  443.4 30.3 %all-reduce.6.cloned.1.call-done = bf16[192,256]{1,0:T(8,128)(2,1)} async-done(((bf16[192,256]{1,0:T(8,128)(2,1)}), bf16[192,256]{1,0:T(8,128)(2,1)}) %all-reduce.6.cloned.1.call-update) | async-done | bytes 98320 | tf_op jit(solution)/shard_map/psum | solution.py:35
  473.6 5.3 convolution_negate_fusion
  479.0 60.6 %reduce-scatter.2.cloned.1.call-done = f32[64,3072]{1,0:T(8,128)} async-done(((f32[256,3072]{1,0:T(8,128)}), f32[64,3072]{1,0:T(8,128)}) %reduce-scatter.2.cloned.1.call-update) | async-done | bytes 786448 | tf_op jit(solution)/shard_map/reduce_scatter | solution.py:37
  539.5 1.9 convert_element_type.49
  (52 shorter events, 4.3 us)
Async XLA Ops:
  7.2 94.5 %all-gather.4.cloned.1.call-start = ((), (), s32[]{:S(2)}) async-start(), calls=%async_computation.1 | async-start | bytes 5898240 | tf_op jit(solution)/shard_map/all_gather | solution.py:16
  7.9 130.0 %all-reduce.4.cloned.1.call-start = ((), (), s32[]{:S(2)}) async-start(), calls=%async_computation.2 | async-start | bytes 589824 | tf_op jit(solution)/shard_map/psum | solution.py:24
  106.9 83.2 %all-gather.6.cloned.1.call-start = ((), (), s32[]{:S(2)}) async-start(), calls=%async_computation.3 | async-start | bytes 2949120 | tf_op jit(solution)/shard_map/all_gather | solution.py:25
  139.7 299.6 %all-gather.8.cloned.1.call-start = ((), (), s32[]{:S(2)}) async-start(), calls=%async_computation.4 | async-start | bytes 1966080 | tf_op jit(solution)/shard_map/all_gather | solution.py:17
  140.3 333.4 %all-reduce.6.cloned.1.call-start = ((), (), s32[]{:S(2)}) async-start(), calls=%async_computation.5 | async-start | bytes 196608 | tf_op jit(solution)/shard_map/psum | solution.py:35
  199.0 1.5 copy-start.1
  340.0 85.0 %copy-start = (f32[768,768]{1,0:T(8,128)S(1)}, f32[768,768]{1,0:T(8,128)}, u32[]{:S(2)}) copy-start(f32[768,768]{1,0:T(8,128)} %fusion.24) | copy-start | bytes 7077892
  421.7 2.8 copy-start.2
  427.1 7.9 %slice-start = ((s8[4718592]{0:T(1024)(128)(4,1)}), s8[4194304]{0:T(1024)(128)(4,1)S(1)}, s32[]{:S(2)}) async-start(s8[4718592]{0:T(1024)(128)(4,1)} %bitcast.83), calls=%async_computation.7 | async-start | bytes 8388608
  429.6 5.4 slice-start.1
  431.6 3.4 copy-start.3
  443.1 96.4 %reduce-scatter.2.cloned.1.call-start = ((), (), s32[]{:S(2)}) async-start(), calls=%async_computation.6 | async-start | bytes 3932160 | tf_op jit(solution)/shard_map/reduce_scatter | solution.py:37
Sparse Core Ops, SparseCore 0:
  9.5 92.1 all-gather.3
  107.0 30.8 all-reduce.3
  140.0 49.9 all-gather.5
  191.4 35.7 all-gather.7
  443.2 30.3 all-reduce.5
  479.1 60.3 reduce-scatter.1
where the time goes:
time: 552 us; the launch traced here: 549 us
  waiting for transfers between devices  265 us (48%)
  other arithmetic  195 us (35%)
  matrix products  41.5 us (8%)
  local copies, waits for them, and re-layouts  28.2 us (5%)
  between operations  18.6 us (3%)
    another operation x22, other arithmetic, shards(): factor = jnp.linalg.cholesky(margin)  124 us
    all_gather x1, waiting for transfers between devices, shards(): lax.all_gather(orbitals, 'band', axis=0, tiled=True)  93.7 us
    another operation x3, other arithmetic, shards(): lax.linalg.triangular_solve(factor, identity, left_side=True, lower=True)  62 us
    reduce_scatter x1, waiting for transfers between devices, shards(): lax.psum_scatter(-contract_first(coupling, projector), 'band', scatter_di...  60.6 us
    all_gather x1, waiting for transfers between devices, shards(): lax.all_gather(summed_rows, 'band', axis=0, tiled=True)  47.9 us
    psum x1, waiting for transfers between devices, shards(): lax.psum(partial_rows.astype(jnp.bfloat16), 'ga').astype(jnp.float32)  30.9 us
    psum x1, waiting for transfers between devices, shards(): lax.psum(local_coupling.astype(jnp.bfloat16), 'ga').astype(jnp.float32)  30.3 us
    another operation x18, local copies, waits for them, and re-layouts  21.3 us
  transfers between devices with their start and end apart: 6, of which 5 were waited for; matrix products, arithmetic and copies ran while one was open for 45% of the time, Pallas kernels for 0%

commit v1 on v0

--- a/solution.py
+++ b/solution.py
@@ -22,7 +22,12 @@
         orbitals, weighted, (((1,), (1,)), ((), ())), preferred_element_type=jnp.float32
     )
     summed_rows = lax.psum(partial_rows.astype(jnp.bfloat16), "ga").astype(jnp.float32)
-    margin = -lax.all_gather(summed_rows, "band", axis=0, tiled=True) / total_coeffs
+    margin = (
+        -jnp.concatenate(
+            lax.all_to_all(jnp.stack([summed_rows] * lax.axis_size("band")), "band", 0, 0), axis=0
+        )
+        / total_coeffs
+    )
     factor = jnp.linalg.cholesky(margin)
     identity = jnp.eye(factor.shape[0], dtype=jnp.float32)
     inverse = lax.linalg.triangular_solve(factor, identity, left_side=True, lower=True)

time: 552 us -> 582 us (1.054)
  waiting for transfers between devices: 265 us -> 293 us
    all_to_all x0 -> x1, waiting for transfers between devices: none -> 75.5 us  [shards(): lax.all_to_all(jnp.stack([summed_rows] * lax.axis_size('band')), 'band',...]
    all_gather x1 -> x0, waiting for transfers between devices: 47.9 us -> none  [shards(): lax.all_gather(summed_rows, 'band', axis=0, tiled=True)]
    another operation x18 -> x19, local copies, waits for them, and re-layouts: 21.3 us -> 24.1 us
  transfers between devices with their start and end apart: 6 -> 6, of which waited for: 5 -> 5; matrix products, arithmetic and copies ran while one was open for 45% -> 42% of each run, Pallas kernels for 0% -> 0%
where the time goes in v1:
time: 582 us; the launch traced here: 579 us
  waiting for transfers between devices  293 us (50%)
  other arithmetic  193 us (33%)
  matrix products  41.5 us (7%)
  local copies, waits for them, and re-layouts  28 us (5%)
  between operations  18.2 us (3%)
    another operation x22, other arithmetic, shards(): factor = jnp.linalg.cholesky(margin)  124 us
    all_gather x1, waiting for transfers between devices, shards(): lax.all_gather(orbitals, 'band', axis=0, tiled=True)  93.7 us
    all_to_all x1, waiting for transfers between devices, shards(): lax.all_to_all(jnp.stack([summed_rows] * lax.axis_size('band')), 'band',...  75.5 us
    another operation x3, other arithmetic, shards(): lax.linalg.triangular_solve(factor, identity, left_side=True, lower=True)  62 us
    reduce_scatter x1, waiting for transfers between devices, shards(): lax.psum_scatter(-contract_first(coupling, projector), 'band', scatter_di...  60.6 us
    psum x1, waiting for transfers between devices, shards(): lax.psum(partial_rows.astype(jnp.bfloat16), 'ga').astype(jnp.float32)  31 us
    psum x1, waiting for transfers between devices, shards(): lax.psum(local_coupling.astype(jnp.bfloat16), 'ga').astype(jnp.float32)  30.3 us
    another operation x18, local copies, waits for them, and re-layouts  21.5 us
  transfers between devices with their start and end apart: 6, of which 5 were waited for; matrix products, arithmetic and copies ran while one was open for 42% of the time, Pallas kernels for 0%

profile of v1, /device:TPU:0, one launch (start us, length us, event | category | flops | bytes accessed | tf_op | source)
XLA Modules:
  0.0 578.5 jit_solution(12851269268081294261)
XLA Ops:
  7.2 0.7 all-gather.3.cloned.1.call-update
  7.9 93.7 %all-gather.3.cloned.1.call-done = bf16[768,3072]{1,0:T(8,128)(2,1)} async-done(((bf16[192,3072]{1,0:T(8,128)(2,1)}), bf16[768,3072]{1,0:T(8,128)(2,1)}) %all-gather.3.cloned.1.call-update) | async-done | bytes 4718608 | tf_op jit(solution)/shard_map/all_gather | solution.py:16
  101.7 5.1 fusion.20
  106.9 31.0 %all-reduce.4.cloned.1.call-done = bf16[192,768]{1,0:T(8,128)(2,1)} async-done(((bf16[192,768]{1,0:T(8,128)(2,1)}), bf16[192,768]{1,0:T(8,128)(2,1)}) %all-reduce.4.cloned.1.call-update) | async-done | bytes 294928 | tf_op jit(solution)/shard_map/psum | solution.py:24
  137.8 2.6 stack.2
  140.4 4.6 all-to-all-start
  145.0 0.7 all-gather.5.cloned.1.call-update
  146.0 1.6 fusion.24
  147.6 75.5 %all-to-all-done = f32[4,192,768]{2,1,0:T(8,128)} async-done(((f32[4,192,768]{2,1,0:T(8,128)}), f32[4,192,768]{2,1,0:T(8,128)}, u32[]{:S(2)}, u32[]{:S(2)}) %all-to-all-start) | async-done | bytes 2359328 | tf_op jit(solution)/shard_map/all_to_all | solution.py:27
  223.2 1.9 negate_multiply_fusion
  225.0 2.2 copy.7
  227.2 1.9 fusion.2
  229.1 1.5 copy-done.1
  230.6 11.7 %cholesky.165 = f32[128,128]{1,0:T(8,128)S(1)} custom-call(f32[128,128]{1,0:T(8,128)S(1)} %cholesky.424), custom_call_target="Cholesky" | custom-call | tf_op jit(solution)/shard_map/jit(cholesky)/cholesky | solution.py:31
  242.3 9.8 %custom-call.46 = f32[1,128,128]{1,2,0:T(8,128)S(1)} custom-call(f32[1,128,128]{2,1,0:T(8,128)S(1)} %get-tuple-element.45), custom_call_target="InvertDiagBlocksLowerTriangular" | custom-call | tf_op jit(solution)/shard_map/jit(cholesky)/cholesky | solution.py:31
  252.3 1.4 constant_dynamic-update-slice_fusion.15
  253.7 1.4 convolution_subtract_fusion.4
  255.1 11.7 %cholesky.188 = f32[128,128]{1,0:T(8,128)S(1)} custom-call(f32[128,128]{1,0:T(8,128)S(1)} %cholesky.428), custom_call_target="Cholesky" | custom-call | tf_op jit(solution)/shard_map/jit(cholesky)/cholesky | solution.py:31
  266.9 10.0 %custom-call.47 = f32[1,128,128]{1,2,0:T(8,128)S(1)} custom-call(f32[1,128,128]{2,1,0:T(8,128)S(1)} %get-tuple-element.42), custom_call_target="InvertDiagBlocksLowerTriangular" | custom-call | tf_op jit(solution)/shard_map/jit(cholesky)/cholesky | solution.py:31
  277.3 1.5 convolution_subtract_fusion.5
  278.8 11.7 %cholesky.354 = f32[128,128]{1,0:T(8,128)S(1)} custom-call(f32[128,128]{1,0:T(8,128)S(1)} %cholesky.433), custom_call_target="Cholesky" | custom-call | tf_op jit(solution)/shard_map/jit(cholesky)/cholesky | solution.py:31
  290.6 0.7 compare_reduce_fusion.3
  291.3 9.8 %custom-call.48 = f32[1,128,128]{1,2,0:T(8,128)S(1)} custom-call(f32[1,128,128]{2,1,0:T(8,128)S(1)} %get-tuple-element.39), custom_call_target="InvertDiagBlocksLowerTriangular" | custom-call | tf_op jit(solution)/shard_map/jit(cholesky)/cholesky | solution.py:31
  301.4 1.6 convolution_subtract_fusion.6
  303.0 12.2 %cholesky.373 = f32[128,128]{1,0:T(8,128)S(1)} custom-call(f32[128,128]{1,0:T(8,128)S(1)} %cholesky.438), custom_call_target="Cholesky" | custom-call | tf_op jit(solution)/shard_map/jit(cholesky)/cholesky | solution.py:31
  315.2 0.7 compare_reduce_fusion.2
  315.9 9.8 %custom-call.49 = f32[1,128,128]{1,2,0:T(8,128)S(1)} custom-call(f32[1,128,128]{2,1,0:T(8,128)S(1)} %get-tuple-element.36), custom_call_target="InvertDiagBlocksLowerTriangular" | custom-call | tf_op jit(solution)/shard_map/jit(cholesky)/cholesky | solution.py:31
  325.9 1.5 convolution_subtract_fusion.7
  327.5 11.7 %cholesky.392 = f32[128,128]{1,0:T(8,128)S(1)} custom-call(f32[128,128]{1,0:T(8,128)S(1)} %cholesky.443), custom_call_target="Cholesky" | custom-call | tf_op jit(solution)/shard_map/jit(cholesky)/cholesky | solution.py:31
  339.2 0.7 compare_reduce_fusion.1
  339.9 9.8 %custom-call.50 = f32[1,128,128]{1,2,0:T(8,128)S(1)} custom-call(f32[1,128,128]{2,1,0:T(8,128)S(1)} %get-tuple-element.33), custom_call_target="InvertDiagBlocksLowerTriangular" | custom-call | tf_op jit(solution)/shard_map/jit(cholesky)/cholesky | solution.py:31
  349.9 1.3 convolution_subtract_fusion.8
  351.3 11.9 %cholesky.410 = f32[128,128]{1,0:T(8,128)S(1)} custom-call(f32[128,128]{1,0:T(8,128)S(1)} %convolution_subtract_fusion.8), custom_call_target="Cholesky" | custom-call | tf_op jit(solution)/shard_map/jit(cholesky)/cholesky | solution.py:31
  363.2 0.7 compare_reduce_fusion
  363.9 0.7 compare_reduce_fusion.4
  368.4 1.6 select_select_fusion
  370.1 21.5 %while.1 = (s32[]{:T(128)}, f32[768,768]{1,0:T(8,128)}, s32[6,2]{0,1:T(2,128)S(1)}, f32[6,128,128]{2,1,0:T(8,128)}, s32[]{:T(128)}) while((s32[]{:T(128)}, f32[768,768]{1,0:T(8,128)}, s32[6,2]{0,1:T(2,128)S(1)}, f32[6,128,128]{2,1,0:T(8,128)}, s32[]{:T(128)}) %tuple.45), condition=%wide.while_cond, body=%wide.while_body.sunk | while | flops 2 | bytes 132705 | solution.py:33
  370.1 0.6 fusion.79
  370.7 3.0 bitcast_dynamic-update-slice_fusion.2
  373.8 0.6 fusion.79
  374.4 2.9 bitcast_dynamic-update-slice_fusion.2
  377.4 0.6 fusion.79
  378.0 2.9 bitcast_dynamic-update-slice_fusion.2
  381.0 0.6 fusion.79
  381.6 2.9 bitcast_dynamic-update-slice_fusion.2
  384.6 0.6 fusion.79
  385.1 2.9 bitcast_dynamic-update-slice_fusion.2
  388.2 0.6 fusion.79
  388.7 2.9 bitcast_dynamic-update-slice_fusion.2
  391.6 60.4 %custom-call.51 = f32[6,128,128]{1,2,0:T(8,128)} custom-call(f32[6,128,128]{2,1,0:T(8,128)} %get-tuple-element.9), custom_call_target="InvertDiagBlocksLowerTriangular" | custom-call | tf_op jit(solution)/shard_map/triangular_solve | solution.py:33
  452.0 1.3 constant_dynamic-update-slice_fusion.4
  453.3 1.5 convolution_subtract_fusion.2
  455.4 1.5 convolution_subtract_fusion.3
  456.9 0.5 constant_dynamic-update-slice_fusion.2
  457.4 2.0 convolution_subtract_fusion.1
  459.4 0.5 constant_dynamic-update-slice_fusion.1
  459.9 2.0 fusion.12
  462.5 2.3 convolution_subtract_fusion
  465.3 4.2 fusion.65
  469.6 3.8 convolution_convert_fusion
  473.7 30.3 %all-reduce.6.cloned.1.call-done = bf16[192,256]{1,0:T(8,128)(2,1)} async-done(((bf16[192,256]{1,0:T(8,128)(2,1)}), bf16[192,256]{1,0:T(8,128)(2,1)}) %all-reduce.6.cloned.1.call-update) | async-done | bytes 98320 | tf_op jit(solution)/shard_map/psum | solution.py:40
  504.0 5.3 convolution_negate_fusion
  509.3 60.6 %reduce-scatter.2.cloned.1.call-done = f32[64,3072]{1,0:T(8,128)} async-done(((f32[256,3072]{1,0:T(8,128)}), f32[64,3072]{1,0:T(8,128)}) %reduce-scatter.2.cloned.1.call-update) | async-done | bytes 786448 | tf_op jit(solution)/shard_map/reduce_scatter | solution.py:42
  569.8 1.9 convert_element_type.49
  (50 shorter events, 4.2 us)
Async XLA Ops:
  7.2 94.5 %all-gather.3.cloned.1.call-start = ((), (), s32[]{:S(2)}) async-start(), calls=%async_computation.2 | async-start | bytes 5898240 | tf_op jit(solution)/shard_map/all_gather | solution.py:16
  7.9 130.0 %all-reduce.4.cloned.1.call-start = ((), (), s32[]{:S(2)}) async-start(), calls=%async_computation.3 | async-start | bytes 589824 | tf_op jit(solution)/shard_map/psum | solution.py:24
  140.4 82.7 %all-to-all-start = ((f32[4,192,768]{2,1,0:T(8,128)}), f32[4,192,768]{2,1,0:T(8,128)}, u32[]{:S(2)}, u32[]{:S(2)}) async-start(f32[4,192,768]{2,1,0:T(8,128)} %stack.2), calls=%async_computation | async-start | bytes 4718592 | tf_op jit(solution)/shard_map/all_to_all | solution.py:27
  145.0 324.6 %all-gather.5.cloned.1.call-start = ((), (), s32[]{:S(2)}) async-start(), calls=%async_computation.4 | async-start | bytes 1966080 | tf_op jit(solution)/shard_map/all_gather | solution.py:17
  145.8 358.2 %all-reduce.6.cloned.1.call-start = ((), (), s32[]{:S(2)}) async-start(), calls=%async_computation.5 | async-start | bytes 196608 | tf_op jit(solution)/shard_map/psum | solution.py:40
  229.1 1.5 copy-start.1
  370.1 85.3 %copy-start = (f32[768,768]{1,0:T(8,128)S(1)}, f32[768,768]{1,0:T(8,128)}, u32[]{:S(2)}) copy-start(f32[768,768]{1,0:T(8,128)} %fusion.24) | copy-start | bytes 7077892
  452.0 2.8 copy-start.2
  457.4 7.9 %slice-start = ((s8[4718592]{0:T(1024)(128)(4,1)}), s8[4194304]{0:T(1024)(128)(4,1)S(1)}, s32[]{:S(2)}) async-start(s8[4718592]{0:T(1024)(128)(4,1)} %bitcast.86), calls=%async_computation.7 | async-start | bytes 8388608
  459.9 5.4 slice-start.1
  461.9 3.4 copy-start.3
  473.4 96.4 %reduce-scatter.2.cloned.1.call-start = ((), (), s32[]{:S(2)}) async-start(), calls=%async_computation.6 | async-start | bytes 3932160 | tf_op jit(solution)/shard_map/reduce_scatter | solution.py:42
Sparse Core Ops, SparseCore 0:
  9.5 92.1 all-gather.2
  107.0 30.8 all-reduce.3
  147.4 63.6 all-gather.4
  473.5 30.3 all-reduce.5
  509.4 60.3 reduce-scatter.1
